TPU v7x, 256 devices: a whole 4x4x8 slice. The times are simulated.
256 devices in a mesh: band: 4 (over x_lo, core), fft: 64 (over y, z, x_hi).
Axes of the slice: x: 4 (x_hi: 2, x_lo: 2; x = x_hi * 2 + x_lo), y: 4, z: 8, core: 2. Of those that a mesh axis runs over, the one named last changes fastest.
Arguments:
- orbitals: bfloat16 [16, 2, 262144], P('band', None, 'fft'), may hold values from -6 to 6
- sphere_slot: int32 [262144], P('fft'), may hold values from 0 to 24575, as said below
- stick_column: int32 [8192], P('fft'), may hold values from 0 to 36863, as said below
- potential: float32 [192, 192, 192], P('fft'), may hold values from -3 to 3
- subspace: bfloat16 [64, 2, 262144], P('band', None, 'fft'), may hold values from -0.0234375 to 0.0234375
- previous: bfloat16 [16, 2, 262144], P('band', None, 'fft'), may hold values from -6 to 6
Outputs:
- applied: bfloat16 [16, 2, 262144], P('band', None, 'fft')
- intersection: float32 [2, 64, 16], P(None, 'fft', 'band')
Inputs may be any that keep to these rules, and one draw needn't show every extreme that they name: `sphere_slot`: within each aligned block of 4096 entries the values are distinct. `stick_column`: aligned block d of 128 entries holds distinct columns x * 192 + y with d * 3 <= x < (d + 1) * 3.
All inputs are finite; a program needn't handle non-finite values.
Results may differ from a plain program's by a relative error of at most 0.012.
Values may be sent and summed in bfloat16 or wider, within the bound.
A program may use at most 64 MiB of HBM per device.

v0:
```python
import functools
import math

import jax
import jax.numpy as jnp
import numpy as np
from jax import lax
from jax.experimental import pallas as pl
from jax.experimental.pallas import tpu as pltpu
from jax.sharding import PartitionSpec as P

F32 = jnp.float32
BF16 = jnp.bfloat16
NT = (((1,), (1,)), ((), ()))


def dot(a, b):
    return jnp.dot(a, b, preferred_element_type=F32)


def dot_nt(a, b):
    return lax.dot_general(a, b, NT, preferred_element_type=F32)


def tables(grid, owners):
    depth = grid // owners
    groups = owners // 4
    k = np.arange(grid)
    angle = 2.0 * math.pi * ((k[:, None] * k[None, :]) % grid) / grid
    cos, sin = np.cos(angle), np.sin(angle)
    icos, isin = cos / grid, -sin / grid
    zorder = np.arange(grid)
    zorder = (zorder % owners) * depth + zorder // owners
    rows = np.full(groups * 16, -1)
    for g in range(groups):
        rows[16 * g : 16 * g + 4 * depth] = 4 * depth * g + np.arange(4 * depth)

    def padded(table):
        out = np.zeros((groups * 16, grid))
        out[rows >= 0] = table[rows[rows >= 0]]
        return out

    def trio(c, s):
        return [jnp.asarray(t, BF16) for t in (c, s, -s)]

    zf = trio(cos[zorder], sin[zorder])
    zb = trio(icos[zorder], isin[zorder])
    yf = trio(cos, sin)
    yb = trio(icos, isin)
    xf = trio(padded(cos).T, padded(sin).T)
    xb = trio(padded(icos), padded(isin))
    return zf, zb, yf, yb, xf, xb


def vmem():
    return pl.BlockSpec(memory_space=pltpu.VMEM)


def hot(rows, index, kind=BF16):
    lanes = index.shape[1]
    return (lax.broadcasted_iota(jnp.int32, (rows, lanes), 0) == index).astype(F32).astype(kind)


def frequency(values, grid):
    return jnp.where(values >= grid // 2, values - grid, values).astype(F32)


def start_to(src, dst, send_sem, recv_sem, axis, peer):
    pltpu.make_async_remote_copy(
        src_ref=src,
        dst_ref=dst,
        send_sem=send_sem,
        recv_sem=recv_sem,
        device_id={axis: peer},
        device_id_type=pl.DeviceIdType.MESH,
    ).start()


def wait_bytes(ref, sem):
    pltpu.make_async_copy(ref, ref, sem).wait()


def others(axis, count, act):
    me = lax.axis_index(axis)

    def step(j, carry):
        act(me, lax.rem(me + j, count))
        return carry

    lax.fori_loop(1, count, step, 0)


def kernel(dims, *refs):
    owners, groups, grid, depth, sticks, waves, bands, teams, subs = dims
    orb, slot, column, pot, sub, prev = refs[:6]
    zf, zb, yf, yb, xf, xb = (refs[6 + 3 * i : 9 + 3 * i] for i in range(6))
    out, inter = refs[24:26]
    (stick_hot, plane_hot, rep, lhs, stage, send, recv, send2, recv2, cols, ymask, ymask_t, xmask,
     val, gre, gim, back, pall, r1, r2, r3) = refs[26:47]
    col_s, col_r, fwd_s, fwd_r, bwd_s, bwd_r, prev_s, prev_r, one_s, one_r, two_s, two_r = refs[47:]
    parts = 2 * bands
    wide = 4 * sticks
    chunk = 512
    me = lax.axis_index("fft")
    team = lax.axis_index("band")

    barrier = pltpu.get_barrier_semaphore()

    def greet(axis):
        def act(own, peer):
            pl.semaphore_signal(
                barrier, inc=1, device_id={axis: peer}, device_id_type=pl.DeviceIdType.MESH
            )

        return act

    others("fft", owners, greet("fft"))
    others("band", teams, greet("band"))

    for c in range(0, waves, chunk):
        cut = slice(c, c + chunk)
        sl = slot[:, cut]
        stick_hot[:, cut] = hot(sticks, lax.rem(sl, sticks))
        plane_hot[:, cut] = hot(grid, lax.div(sl, sticks))
        for r in range(parts):
            row = orb[r : r + 1, cut].astype(F32)
            rep[r, :, cut] = jnp.broadcast_to(row, (16, chunk)).astype(BF16)

    pl.semaphore_wait(barrier, owners + teams - 2)
    others("fft", owners, lambda own, peer: start_to(
        column, cols.at[own], col_s, col_r, "fft", peer))
    pltpu.make_async_copy(column, cols.at[me], col_r).start()
    others("band", teams, lambda own, peer: start_to(
        prev, pall.at[own], prev_s, prev_r, "band", peer))
    pltpu.make_async_copy(prev, pall.at[team], prev_r).start()

    zc, zs, zn = (t[...] for t in zf)
    for h in range(parts // 4):
        for r in range(4):
            lhs[sticks * r : sticks * (r + 1), :] = (
                stick_hot[...].reshape(sticks // 16, 16, waves) * rep[4 * h + r][None]
            ).reshape(sticks, waves)
        got = dot_nt(lhs[...], plane_hot[...]).astype(BF16)
        for k in range(2):
            b = 2 * h + k
            re = got[2 * k * sticks : (2 * k + 1) * sticks]
            im = got[(2 * k + 1) * sticks : (2 * k + 2) * sticks]
            pair = (
                dot_nt(zc, re) + dot_nt(zn, im),
                dot_nt(zs, re) + dot_nt(zc, im),
            )
            for p in range(2):
                for z in range(depth):
                    rows = pl.ds(p * bands + b, owners, stride=parts)
                    stage[z, rows, :] = pair[p][z * owners : (z + 1) * owners]
    for z in range(depth):
        for f in range(owners):
            send[z, f] = stage[z, parts * f : parts * (f + 1), :].astype(BF16)
    for z in range(depth):
        others("fft", owners, lambda own, peer, z=z: start_to(
            send.at[z, peer], recv.at[z, own], fwd_s.at[z], fwd_r.at[z], "fft", peer))
        pltpu.make_async_copy(send.at[z, me], recv.at[z, me], fwd_r.at[z]).start()

    wait_bytes(cols, col_r)
    for g in range(groups):
        for d in range(4):
            col = cols[4 * g + d]
            x = lax.div(col, grid)
            y = col - x * grid
            x = x - 4 * depth * g
            lanes = slice(sticks * d, sticks * (d + 1))
            ymask[g, :, lanes] = hot(grid, y)
            xmask[g, :, lanes] = hot(16, x, F32)
            yt = jnp.broadcast_to(y.astype(F32), (sticks, sticks)).T.astype(jnp.int32)
            wide_y = jnp.concatenate([yt, yt], axis=1)[:, :grid]
            ymask_t[g, lanes, :] = (
                lax.broadcasted_iota(jnp.int32, (sticks, grid), 1) == wide_y
            ).astype(F32).astype(BF16)

    wait_bytes(pall, prev_r)
    for t in range(teams):
        part = lax.dot_general(sub[...], pall[t], NT, preferred_element_type=F32)
        part = jnp.concatenate([part, jnp.zeros((2 * subs, 128 - parts), F32)], axis=1)
        for j in range(subs):
            r1[t, j] = part[2 * j : 2 * j + 2, :]
    others("band", teams, lambda own, peer: start_to(
        r1.at[peer], r2.at[own], one_s, one_r, "band", peer))
    pltpu.make_async_copy(r1.at[team], r2.at[team], one_r).start()

    def plane(z, carry):
        wait_bytes(recv.at[z], fwd_r.at[z])

        def scatter(g, carry):
            for d in range(4):
                val[g, :, sticks * d : sticks * (d + 1)] = recv[z, 4 * g + d].astype(F32)
            mask = xmask[g]
            block = jnp.concatenate(
                [(mask * val[g, r : r + 1, :]).astype(BF16) for r in range(parts)], axis=0
            )
            got = dot(block, ymask_t[g]).astype(BF16)
            at = pl.ds(pl.multiple_of(16 * g, 16), 16)
            gre[:, at, :] = got[: bands * 16].reshape(bands, 16, grid)
            gim[:, at, :] = got[bands * 16 :].reshape(bands, 16, grid)
            return carry

        lax.fori_loop(0, groups, scatter, 0, unroll=4)

        def local(b, carry):
            v = pot[z]
            re, im = gre[b], gim[b]
            yr = (dot(re, yf[0][...]) + dot(im, yf[2][...])).astype(BF16)
            yi = (dot(re, yf[1][...]) + dot(im, yf[0][...])).astype(BF16)
            wr = ((dot(xf[0][...], yr) + dot(xf[2][...], yi)) * v).astype(BF16)
            wi = ((dot(xf[1][...], yr) + dot(xf[0][...], yi)) * v).astype(BF16)
            br = (dot(xb[0][...], wr) + dot(xb[2][...], wi)).astype(BF16)
            bi = (dot(xb[1][...], wr) + dot(xb[0][...], wi)).astype(BF16)
            back[b] = (dot(br, yb[0][...]) + dot(bi, yb[2][...])).astype(BF16)
            back[bands + b] = (dot(br, yb[1][...]) + dot(bi, yb[0][...])).astype(BF16)
            return carry

        lax.fori_loop(0, bands, local, 0, unroll=2)

        def pick(g, carry):
            at = pl.ds(pl.multiple_of(16 * g, 16), 16)
            block = back[:, at, :].reshape(parts * 16, grid)
            t = dot(block, ymask[g]).reshape(parts, 16, wide)
            got = jnp.sum(t * xmask[g][None], axis=1)
            for d in range(4):
                send2[z, 4 * g + d] = got[:, sticks * d : sticks * (d + 1)].astype(BF16)
            return carry

        lax.fori_loop(0, groups, pick, 0, unroll=4)
        others("fft", owners, lambda own, peer: start_to(
            send2.at[z, peer], recv2.at[z, own], bwd_s.at[z], bwd_r.at[z], "fft", peer))
        pltpu.make_async_copy(send2.at[z, me], recv2.at[z, me], bwd_r.at[z]).start()
        return carry

    plane(0, 0)
    wait_bytes(r2, one_r)
    others("fft", owners, lambda own, peer: start_to(
        r2.at[lax.div(peer, subs), lax.rem(peer, subs)], r3.at[own], two_s, two_r, "fft", peer))
    pltpu.make_async_copy(
        r2.at[lax.div(me, subs), lax.rem(me, subs)], r3.at[me], two_r).start()
    lax.fori_loop(1, depth, plane, 0)

    wait_bytes(r3, two_r)
    total = jnp.sum(r3[...], axis=0)
    inter[...] = total

    col = column[...]
    x = lax.div(col, grid)
    y = col - x * grid
    coords = jnp.concatenate([x, y, x, y, x, y, x, y], axis=0).astype(F32).astype(BF16)
    for z in range(depth):
        wait_bytes(recv2.at[z], bwd_r.at[z])
        for f in range(owners):
            stage[z, parts * f : parts * (f + 1), :] = recv2[z, f].astype(F32)
    zc, zs, zn = (t[...] for t in zb)
    lines = []
    for b in range(bands):
        pair = []
        for p in range(2):
            rows = pl.ds(p * bands + b, owners, stride=parts)
            pair.append(
                jnp.concatenate([stage[z, rows, :] for z in range(depth)], axis=0).T.astype(BF16)
            )
        re, im = pair
        lines.append((dot(re, zc) + dot(im, zn)).astype(BF16))
        lines.append((dot(re, zs) + dot(im, zc)).astype(BF16))
    lines = jnp.concatenate(lines, axis=0)
    for c in range(0, waves, chunk):
        cut = slice(c, c + chunk)
        plane_at = lax.div(slot[:, cut], sticks)
        shot = stick_hot[:, cut]
        xy = dot(coords, shot)
        fz = frequency(plane_at, grid)
        fx = frequency(xy[0:1].astype(jnp.int32), grid)
        fy = frequency(xy[1:2].astype(jnp.int32), grid)
        kinetic = (fz * fz + fx * fx + fy * fy) * (2.0 / (grid * grid))
        t = dot(lines, plane_hot[:, cut]).reshape(parts, sticks, chunk)
        got = jnp.sum(t * shot.astype(F32)[None], axis=1)
        out[:, cut] = (got + kinetic * orb[:, cut].astype(F32)).astype(BF16)

    rest = pl.ds(0, owners - 1)
    for z in range(depth):
        wait_bytes(send.at[z, rest], fwd_s.at[z])
        wait_bytes(send2.at[z, rest], bwd_s.at[z])
    wait_bytes(cols.at[rest], col_s)
    wait_bytes(r3.at[rest], two_s)
    wait_bytes(pall.at[pl.ds(0, teams - 1)], prev_s)
    wait_bytes(r1.at[pl.ds(0, teams - 1)], one_s)


def per_device(orbitals, sphere_slot, stick_column, potential, subspace, previous):
    owners = lax.axis_size("fft")
    teams = lax.axis_size("band")
    groups = owners // 4
    depth, grid, _ = potential.shape
    sticks = stick_column.shape[0]
    waves = sphere_slot.shape[0]
    bands = orbitals.shape[0]
    subs = subspace.shape[0]
    parts = 2 * bands
    every = [t for trio in tables(grid, owners) for t in trio]
    dims = (owners, groups, grid, depth, sticks, waves, bands, teams, subs)
    message = pltpu.VMEM((depth, owners, parts, sticks), BF16)
    sums = pltpu.VMEM((teams, subs, 2, 128), F32)
    one = pltpu.SemaphoreType.DMA
    several = pltpu.SemaphoreType.DMA((depth,))
    applied, inter = pl.pallas_call(
        functools.partial(kernel, dims),
        out_shape=[
            jax.ShapeDtypeStruct((parts, waves), BF16),
            jax.ShapeDtypeStruct((2, 128), F32),
        ],
        in_specs=[vmem() for _ in range(6 + len(every))],
        out_specs=[vmem(), vmem()],
        scratch_shapes=[
            pltpu.VMEM((sticks, waves), BF16),
            pltpu.VMEM((grid, waves), BF16),
            pltpu.VMEM((parts, 16, waves), BF16),
            pltpu.VMEM((4 * sticks, waves), BF16),
            pltpu.VMEM((depth, owners * parts, sticks), F32),
            message,
            message,
            message,
            message,
            pltpu.VMEM((owners, 1, sticks), jnp.int32),
            pltpu.VMEM((groups, grid, 4 * sticks), BF16),
            pltpu.VMEM((groups, 4 * sticks, grid), BF16),
            pltpu.VMEM((groups, 16, 4 * sticks), F32),
            pltpu.VMEM((groups, parts, 4 * sticks), F32),
            pltpu.VMEM((bands, groups * 16, grid), BF16),
            pltpu.VMEM((bands, groups * 16, grid), BF16),
            pltpu.VMEM((parts, groups * 16, grid), BF16),
            pltpu.VMEM((teams, parts, waves), BF16),
            sums,
            sums,
            pltpu.VMEM((owners, 2, 128), F32),
            one, one, several, several, several, several, one, one, one, one, one, one,
        ],
        compiler_params=pltpu.CompilerParams(
            vmem_limit_bytes=60 * 2**20, collective_id=0, has_side_effects=True
        ),
        name="apply",
    )(
        orbitals.reshape(parts, waves),
        sphere_slot.reshape(1, waves),
        stick_column.reshape(1, sticks),
        potential,
        subspace.reshape(2 * subs, waves),
        previous.reshape(parts, waves),
        *every,
    )
    sums = inter[:, :parts].reshape(2, bands, 2)
    intersection = jnp.stack(
        [sums[0, :, 0] + sums[1, :, 1], sums[0, :, 1] - sums[1, :, 0]]
    )[:, None]
    return applied.reshape(orbitals.shape), intersection


def solution(mesh):
    return jax.shard_map(
        per_device,
        mesh=mesh,
        in_specs=(
            P("band", None, "fft"),
            P("fft"),
            P("fft"),
            P("fft", None, None),
            P("band", None, "fft"),
            P("band", None, "fft"),
        ),
        out_specs=(P("band", None, "fft"), P(None, "fft", "band")),
        check_vma=False,
    )
```

profile of v0, /device:TPU:8, one launch (start us, length us, event | category | flops | bytes accessed | tf_op | source)
XLA Modules:
  0.0 69.7 jit_solution(8972646009434833218)
XLA Ops:
  0.6 0.0 copy-start
  0.6 1.5 %reshape.61.refs_0_ = bf16[8,4096]{1,0:T(8,128)(2,1)} reshape(bf16[4,2,4096]{2,1,0:T(2,128)(2,1)} %param.24) | data formatting | bytes 131072 | tf_op jit(solution)/shard_map/reshape | solution.py:347
  2.2 1.5 %reshape.65.refs_5_ = bf16[8,4096]{1,0:T(8,128)(2,1)} reshape(bf16[4,2,4096]{2,1,0:T(2,128)(2,1)} %param.29) | data formatting | bytes 131072 | tf_op jit(solution)/shard_map/reshape | solution.py:352
  3.7 0.0 copy-done
  3.7 0.8 %reshape.64.refs_4_ = bf16[32,4096]{1,0:T(8,128)(2,1)} reshape(bf16[16,2,4096]{2,1,0:T(2,128)(2,1)S(1)} %copy-done) | data formatting | bytes 524288 | tf_op jit(solution)/shard_map/reshape | solution.py:351
  4.5 62.2 %apply.1 = (bf16[8,4096]{1,0:T(8,128)(2,1)}, f32[2,128]{1,0:T(2,128)}) custom-call(bf16[8,4096]{1,0:T(8,128)(2,1)} %reshape.61.refs_0_, s32[1,4096]{1,0:T(1,128)} %bitcast.8, s32[1,128]{1,0:T(1,128)} %bitcast.13, f32[3,192,192]{2,1,0:T(8,128)} %refs_3_.1, bf16[32,4096]{1,0:T(8,128)(2,1)} %reshape.64.refs_4_, bf16[8,4096]{1,0:T(8,128)(2,1)} %reshape.65.refs_5_, ...), custom_call_target="tpu_custom_call" | custom-call | tf_op jit(solution)/shard_map/apply/pallas_call | solution.py:310
  66.6 1.5 %reshape.66 = bf16[4,2,4096]{2,1,0:T(2,128)(2,1)} reshape(bf16[8,4096]{1,0:T(8,128)(2,1)} %get-tuple-element.4) | data formatting | bytes 131072 | tf_op jit(solution)/shard_map/reshape | solution.py:359
  68.1 0.0 copy-start.1
  68.1 0.7 copy-done.1
  68.8 0.1 reshape.67
  68.9 0.2 fusion.1
  69.1 0.6 pad_maximum_fusion
Async XLA Ops:
  0.6 3.0 %copy-start = (bf16[16,2,4096]{2,1,0:T(2,128)(2,1)S(1)}, bf16[16,2,4096]{2,1,0:T(2,128)(2,1)}, u32[]{:S(2)}) copy-start(bf16[16,2,4096]{2,1,0:T(2,128)(2,1)} %param.28) | copy-start | bytes 786436
  68.1 0.7 copy-start.1
where the time goes:
time: 69.9 us; the launch traced here: 69.7 us
  Pallas kernels  62.2 us (89%)
  local copies, waits for them, and re-layouts  6.09 us (9%)
  other arithmetic  0.8 us (1%)
    pallas_call x1, Pallas kernels, per_device(): pl.pallas_call(functools.partial(kernel, dims), out_shape=[jax.ShapeDtype...  62.2 us
    reshape x1, local copies, waits for them, and re-layouts, per_device(): orbitals.reshape(parts, waves)  1.54 us
    reshape x1, local copies, waits for them, and re-layouts, per_device(): return (applied.reshape(orbitals.shape), intersection)  1.52 us
    reshape x1, local copies, waits for them, and re-layouts, per_device(): previous.reshape(parts, waves)  1.48 us

commit v1 on v0

v1 whole, which is shorter than its diff:
```python
import functools
import math

import jax
import jax.numpy as jnp
import numpy as np
from jax import lax
from jax.experimental import pallas as pl
from jax.experimental.pallas import tpu as pltpu
from jax.sharding import PartitionSpec as P

F32 = jnp.float32
BF16 = jnp.bfloat16
NT = (((1,), (1,)), ((), ()))


def dot(a, b):
    return jnp.dot(a, b, preferred_element_type=F32)


def dot_nt(a, b):
    return lax.dot_general(a, b, NT, preferred_element_type=F32)


def tables(grid, owners):
    depth = grid // owners
    block = 4 * depth
    half = grid // 2
    lanes = 128
    k = np.arange(grid)
    m = np.arange(half)
    zorder = (k % owners) * depth + k // owners

    def bf16(t):
        return jnp.asarray(t, BF16)

    def waves(rows, cols, sign, scale):
        angle = 2.0 * math.pi * ((rows[:, None] * cols[None, :]) % grid) / grid
        return np.cos(angle) * scale, sign * np.sin(angle) * scale

    def joined(c, s, rows, cols, height, width):
        out = np.zeros((2 * height, 2 * width))
        out[np.ix_(rows, cols)] = c
        out[np.ix_(height + rows, cols)] = -s
        out[np.ix_(rows, width + cols)] = s
        out[np.ix_(height + rows, width + cols)] = c
        return out

    xpos = 16 * (m // block) + m % block
    wide = groups16(owners) // 2
    order = np.concatenate([k[0::2], k[1::2]])
    zf = waves(zorder, order, 1.0, 1.0)
    zb = waves(order, zorder, -1.0, 1.0 / grid)
    made = [np.concatenate([zf[0], -zf[1]], 1), np.concatenate([zf[1], zf[0]], 1)]
    made += [np.concatenate([zb[0], -zb[1]], 1), np.concatenate([zb[1], zb[0]], 1)]
    for odd in range(2):
        made.append(joined(*waves(m, 2 * m + odd, 1.0, 1.0), m, m, lanes, lanes))
    for odd in range(2):
        made.append(joined(*waves(m, 2 * m + odd, 1.0, 1.0), xpos, m, wide, half).T)
    for odd in range(2):
        made.append(joined(*waves(2 * m + odd, m, -1.0, 1.0 / grid), m, xpos, half, wide).T)
    for odd in range(2):
        made.append(joined(*waves(2 * m + odd, m, -1.0, 1.0 / grid), m, m, lanes, lanes))
    return [bf16(t) for t in made]


def groups16(owners):
    return owners // 4 * 16


def vmem():
    return pl.BlockSpec(memory_space=pltpu.VMEM)


def hot(rows, index, kind=BF16):
    lanes = index.shape[1]
    return (lax.broadcasted_iota(jnp.int32, (rows, lanes), 0) == index).astype(F32).astype(kind)


def frequency(values, grid):
    return jnp.where(values >= grid // 2, values - grid, values).astype(F32)


def start_to(src, dst, send_sem, recv_sem, axis, peer):
    pltpu.make_async_remote_copy(
        src_ref=src,
        dst_ref=dst,
        send_sem=send_sem,
        recv_sem=recv_sem,
        device_id={axis: peer},
        device_id_type=pl.DeviceIdType.MESH,
    ).start()


def wait_bytes(ref, sem):
    pltpu.make_async_copy(ref, ref, sem).wait()


def others(axis, count, act):
    me = lax.axis_index(axis)

    def step(j, carry):
        act(me, lax.rem(me + j, count))
        return carry

    lax.fori_loop(1, count, step, 0, unroll=3)


def kernel(dims, *refs):
    owners, groups, grid, depth, sticks, waves, bands, teams, subs = dims
    orb, slot, column, pot, sub, prev = refs[:6]
    zf, zb, yf, xf, xb, yb = (refs[6 + 2 * i : 8 + 2 * i] for i in range(6))
    out, inter = refs[18:20]
    (high_hot, low_hot, rep, stage, send, recv, send2, recv2, cols, ymask, ymask_t, xmask,
     val, gre, gim, back, pots, turn, pall, r1, r2, r3) = refs[20:42]
    col_s, col_r, fwd_s, fwd_r, bwd_s, bwd_r, prev_s, prev_r, one_s, one_r, two_s, two_r = refs[42:]
    parts = 2 * bands
    wide = 4 * sticks
    half = grid // 2
    low = 2 * sticks
    rows = groups * 16
    mid = rows // 2
    chunk = 512
    me = lax.axis_index("fft")
    team = lax.axis_index("band")

    barrier = pltpu.get_barrier_semaphore()

    def greet(axis):
        def act(own, peer):
            pl.semaphore_signal(
                barrier, inc=1, device_id={axis: peer}, device_id_type=pl.DeviceIdType.MESH
            )

        return act

    others("fft", owners, greet("fft"))
    others("band", teams, greet("band"))

    with jax.named_scope("hots"):
        for c in range(0, waves, chunk):
            cut = slice(c, c + chunk)
            sl = slot[:, cut]
            high_hot[:, cut] = hot(half, lax.div(sl, low))
            low_hot[:, cut] = hot(low, lax.rem(sl, low))
            for b in range(bands):
                pair = orb[b, :, cut].astype(F32)
                for p in range(2):
                    rep[2 * b + p, :, cut] = jnp.broadcast_to(pair[p : p + 1], (16, chunk)).astype(BF16)

    with jax.named_scope("barrier"):
        pl.semaphore_wait(barrier, owners + teams - 2)
        others("fft", owners, lambda own, peer: start_to(
            column, cols.at[own], col_s, col_r, "fft", peer))
        pltpu.make_async_copy(column, cols.at[me], col_r).start()
        others("band", teams, lambda own, peer: start_to(
            prev, pall.at[own], prev_s, prev_r, "band", peer))
        pltpu.make_async_copy(prev, pall.at[team], prev_r).start()

    with jax.named_scope("zdft"):
        got = None
        for c in range(0, waves, chunk):
            cut = slice(c, c + chunk)
            high = high_hot[:, cut].reshape(half // 16, 16, chunk)
            block = jnp.concatenate(
                [(high * rep[r, :, cut][None]).reshape(half, chunk) for r in range(parts)], axis=0
            )
            piece = dot_nt(block, low_hot[:, cut])
            got = piece if got is None else got + piece
        got = got.astype(BF16)
        for b in range(bands):
            cut = got[2 * b * half : 2 * (b + 1) * half]
            field = jnp.concatenate(
                [cut[p * half : (p + 1) * half, q * sticks : (q + 1) * sticks]
                 for p in range(2) for q in range(2)], axis=0
            )
            for p in range(2):
                done = dot(zf[p][...], field)
                for z in range(depth):
                    at = pl.ds(p * bands + b, owners, stride=parts)
                    stage[z, at, :] = done[z * owners : (z + 1) * owners]
        for z in range(depth):
            for f in range(owners):
                send[z, f] = stage[z, parts * f : parts * (f + 1), :].astype(BF16)
    with jax.named_scope("sends"):
        for z in range(depth):
            others("fft", owners, lambda own, peer, z=z: start_to(
                send.at[z, peer], recv.at[z, own], fwd_s.at[z], fwd_r.at[z], "fft", peer))
            pltpu.make_async_copy(send.at[z, me], recv.at[z, me], fwd_r.at[z]).start()

    with jax.named_scope("masks"):
        wait_bytes(cols, col_r)
        for g in range(groups):
            for d in range(4):
                col = cols[4 * g + d]
                x = lax.div(col, grid)
                y = col - x * grid
                x = x - 4 * depth * g
                y = jnp.where(y >= half, y + (128 - half), y)
                lanes = slice(sticks * d, sticks * (d + 1))
                ymask[g, :, lanes] = hot(256, y)
                xmask[g, :, lanes] = hot(16, x, F32)
                yt = jnp.broadcast_to(y.astype(F32), (sticks, sticks)).T.astype(jnp.int32)
                wide_y = jnp.concatenate([yt, yt], axis=1)
                ymask_t[g, lanes, :] = (
                    lax.broadcasted_iota(jnp.int32, (sticks, 256), 1) == wide_y
                ).astype(F32).astype(BF16)
        side = jnp.zeros((grid, 256 - grid), F32)
        gap = jnp.zeros((128 - half, 256), F32)

        def sorted_rows(table):
            for q in range(2):
                turn[q] = table[:, 128 * q : 128 * (q + 1)]
            return [
                jnp.concatenate([turn[q, pl.ds(odd, half, stride=2), :] for q in range(2)], axis=1)
                for odd in range(2)
            ]

        for z in range(depth):
            even, odd = sorted_rows(jnp.concatenate([pot[z], side], axis=1))
            table = jnp.concatenate([even, odd], axis=0).T[:grid]
            even, odd = sorted_rows(jnp.concatenate([table, side], axis=1))
            pots[z] = jnp.concatenate([even, gap, odd, gap], axis=0).T[:grid]

    with jax.named_scope("inter1"):
        wait_bytes(pall, prev_r)
        left = jnp.concatenate([sub[j] for j in range(subs)], axis=0)
        for t in range(teams):
            right = jnp.concatenate(
                [pall[t, i][p : p + 1] for p in range(2) for i in range(bands)], axis=0
            )
            part = dot_nt(left, right)
            part = jnp.concatenate([part, jnp.zeros((2 * subs, 128 - parts), F32)], axis=1)
            for j in range(subs):
                r1[t, j] = part[2 * j : 2 * j + 2, :]
        others("band", teams, lambda own, peer: start_to(
            r1.at[peer], r2.at[own], one_s, one_r, "band", peer))
        pltpu.make_async_copy(r1.at[team], r2.at[team], one_r).start()

    def plane(z, carry):
        with jax.named_scope("waitz"):
            wait_bytes(recv.at[z], fwd_r.at[z])

        def scatter(g, carry):
            for d in range(4):
                val[g, :, sticks * d : sticks * (d + 1)] = recv[z, 4 * g + d].astype(F32)
            mask = xmask[g]
            block = jnp.concatenate(
                [(mask * val[g, r : r + 1, :]).astype(BF16) for r in range(parts)], axis=0
            )
            got = dot(block, ymask_t[g]).astype(BF16)
            at = pl.ds(pl.multiple_of(16 * g, 16), 16)
            gre[:, at, :] = got[: bands * 16].reshape(bands, 16, 256)
            gim[:, at, :] = got[bands * 16 :].reshape(bands, 16, 256)
            return carry

        with jax.named_scope("scatter"):
            lax.fori_loop(0, groups, scatter, 0, unroll=4)

        with jax.named_scope("local"):
            local(z)

        def quarter(i, carry):
            q = lax.rem(lax.div(me, 16) + i, owners // 16)
            for k in range(4):
                g = 4 * q + k
                at = pl.ds(pl.multiple_of(16 * g, 16), 16)
                block = back[:, at, :].reshape(parts * 16, 256)
                t = dot(block, ymask[g]).reshape(parts, 16, wide)
                got = jnp.sum(t * xmask[g][None], axis=1)
                for d in range(4):
                    send2[z, 4 * g + d] = got[:, sticks * d : sticks * (d + 1)].astype(BF16)

            def give(j, carry):
                peer = 16 * q + lax.rem(me + j, 16)
                start_to(send2.at[z, peer], recv2.at[z, me], bwd_s.at[z], bwd_r.at[z], "fft", peer)
                return carry

            lax.fori_loop(1, 16, give, 0, unroll=5)

            @pl.when(i > 0)
            def _():
                give(0, 0)

            @pl.when(i == 0)
            def _():
                pltpu.make_async_copy(send2.at[z, me], recv2.at[z, me], bwd_r.at[z]).start()

            return carry

        with jax.named_scope("pick"):
            lax.fori_loop(0, owners // 16, quarter, 0)
        return carry

    def local(z):
        ve, vo = pots[z, :half], pots[z, half:]
        every = range(bands)
        ys = []
        for b in every:
            re, im = gre[b], gim[b]
            a = jnp.concatenate([re[:, :128], im[:, :128]], axis=1)
            c = jnp.concatenate([re[:, 128:], im[:, 128:]], axis=1)
            ys.append((dot(a + c, yf[0][...]).astype(BF16), dot(a - c, yf[1][...]).astype(BF16)))
        xs = []
        for b in every:
            e, o = ys[b]
            re = jnp.concatenate([e[:, :128], o[:, :128]], axis=1)
            im = jnp.concatenate([e[:, 128:], o[:, 128:]], axis=1)
            a = jnp.concatenate([re[:mid], im[:mid]], axis=0)
            c = jnp.concatenate([re[mid:], im[mid:]], axis=0)
            we = (dot(xf[0][...], a + c) * jnp.concatenate([ve, ve], axis=0)).astype(BF16)
            wo = (dot(xf[1][...], a - c) * jnp.concatenate([vo, vo], axis=0)).astype(BF16)
            xs.append((we, wo))
        bs = []
        for b in every:
            e = dot(xb[0][...], xs[b][0])
            o = dot(xb[1][...], xs[b][1])
            bs.append(((e + o).astype(BF16), (e - o).astype(BF16)))
        for b in every:
            p, m = bs[b]
            re = jnp.concatenate([p[:mid], m[:mid]], axis=0)
            im = jnp.concatenate([p[mid:], m[mid:]], axis=0)
            e = dot(jnp.concatenate([re[:, :128], im[:, :128]], axis=1), yb[0][...])
            o = dot(jnp.concatenate([re[:, 128:], im[:, 128:]], axis=1), yb[1][...])
            p, m = (e + o).astype(BF16), (e - o).astype(BF16)
            back[b] = jnp.concatenate([p[:, :128], m[:, :128]], axis=1)
            back[bands + b] = jnp.concatenate([p[:, 128:], m[:, 128:]], axis=1)

    lax.fori_loop(0, depth, plane, 0)

    with jax.named_scope("inter2"):
        wait_bytes(r2, one_r)
        others("fft", owners, lambda own, peer: start_to(
            r2.at[lax.div(peer, subs), lax.rem(peer, subs)], r3.at[own], two_s, two_r, "fft", peer))
        pltpu.make_async_copy(
            r2.at[lax.div(me, subs), lax.rem(me, subs)], r3.at[me], two_r).start()

    with jax.named_scope("waitback"):
        col = column[...]
        x = lax.div(col, grid)
        y = col - x * grid
        coords = jnp.concatenate([x, y, x, y, x, y, x, y], axis=0).astype(F32).astype(BF16)
        coords = jnp.concatenate([coords, coords], axis=1)
        for z in range(depth):
            wait_bytes(recv2.at[z], bwd_r.at[z])
            for f in range(owners):
                stage[z, parts * f : parts * (f + 1), :] = recv2[z, f].astype(F32)
    with jax.named_scope("zback"):
        lines = []
        for b in range(bands):
            field = jnp.concatenate(
                [stage[z, pl.ds(p * bands + b, owners, stride=parts), :].astype(BF16)
                 for p in range(2) for z in range(depth)], axis=0
            )
            for p in range(2):
                done = dot(zb[p][...], field).astype(BF16)
                lines.append(jnp.concatenate([done[:half], done[half:]], axis=1))
        lines = jnp.concatenate(lines, axis=0)
    with jax.named_scope("pickw"):
        for c in range(0, waves, chunk):
            cut = slice(c, c + chunk)
            plane_at = lax.div(slot[:, cut], sticks)
            low_cut = low_hot[:, cut]
            xy = dot(coords, low_cut)
            fz = frequency(plane_at, grid)
            fx = frequency(xy[0:1].astype(jnp.int32), grid)
            fy = frequency(xy[1:2].astype(jnp.int32), grid)
            kinetic = (fz * fz + fx * fx + fy * fy) * (2.0 / (grid * grid))
            t = dot(lines, low_cut).reshape(parts, half, chunk)
            got = jnp.sum(t * high_hot[:, cut].astype(F32)[None], axis=1)
            for b in range(bands):
                out[b, :, cut] = (
                    got[2 * b : 2 * b + 2] + kinetic * orb[b, :, cut].astype(F32)
                ).astype(BF16)

    with jax.named_scope("waits"):
        wait_bytes(r3, two_r)
        total = jnp.sum(r3[...], axis=0)
        moved = pltpu.roll(total, 128 - bands, 1)
        inter[0] = (total[0:1] + moved[1:2])[:, :bands]
        inter[1] = (moved[0:1] - total[1:2])[:, :bands]
        rest = pl.ds(0, owners - 1)
        for z in range(depth):
            wait_bytes(send.at[z, rest], fwd_s.at[z])
            wait_bytes(send2.at[z, rest], bwd_s.at[z])
        wait_bytes(cols.at[rest], col_s)
        wait_bytes(r3.at[rest], two_s)
        wait_bytes(pall.at[pl.ds(0, teams - 1)], prev_s)
        wait_bytes(r1.at[pl.ds(0, teams - 1)], one_s)


def per_device(orbitals, sphere_slot, stick_column, potential, subspace, previous):
    owners = lax.axis_size("fft")
    teams = lax.axis_size("band")
    groups = owners // 4
    depth, grid, _ = potential.shape
    sticks = stick_column.shape[0]
    waves = sphere_slot.shape[0]
    bands = orbitals.shape[0]
    subs = subspace.shape[0]
    parts = 2 * bands
    half = grid // 2
    every = tables(grid, owners)
    dims = (owners, groups, grid, depth, sticks, waves, bands, teams, subs)
    message = pltpu.VMEM((depth, owners, parts, sticks), BF16)
    sums = pltpu.VMEM((teams, subs, 2, 128), F32)
    one = pltpu.SemaphoreType.DMA
    several = pltpu.SemaphoreType.DMA((depth,))
    return tuple(pl.pallas_call(
        functools.partial(kernel, dims),
        out_shape=[
            jax.ShapeDtypeStruct(orbitals.shape, BF16),
            jax.ShapeDtypeStruct((2, 1, bands), F32),
        ],
        in_specs=[vmem() for _ in range(6 + len(every))],
        out_specs=[vmem(), vmem()],
        scratch_shapes=[
            pltpu.VMEM((half, waves), BF16),
            pltpu.VMEM((2 * sticks, waves), BF16),
            pltpu.VMEM((parts, 16, waves), BF16),
            pltpu.VMEM((depth, owners * parts, sticks), F32),
            message,
            message,
            message,
            message,
            pltpu.VMEM((owners, 1, sticks), jnp.int32),
            pltpu.VMEM((groups, 256, 4 * sticks), BF16),
            pltpu.VMEM((groups, 4 * sticks, 256), BF16),
            pltpu.VMEM((groups, 16, 4 * sticks), F32),
            pltpu.VMEM((groups, parts, 4 * sticks), F32),
            pltpu.VMEM((bands, groups * 16, 256), BF16),
            pltpu.VMEM((bands, groups * 16, 256), BF16),
            pltpu.VMEM((parts, groups * 16, 256), BF16),
            pltpu.VMEM((depth, grid, 256), F32),
            pltpu.VMEM((2, grid, 128), F32),
            pltpu.VMEM((teams, *previous.shape), BF16),
            sums,
            sums,
            pltpu.VMEM((owners, 2, 128), F32),
            one, one, several, several, several, several, one, one, one, one, one, one,
        ],
        compiler_params=pltpu.CompilerParams(
            vmem_limit_bytes=60 * 2**20, collective_id=0, has_side_effects=True
        ),
        name="apply",
    )(
        orbitals,
        sphere_slot.reshape(1, waves),
        stick_column.reshape(1, sticks),
        potential,
        subspace,
        previous,
        *every,
    ))


def solution(mesh):
    return jax.shard_map(
        per_device,
        mesh=mesh,
        in_specs=(
            P("band", None, "fft"),
            P("fft"),
            P("fft"),
            P("fft", None, None),
            P("band", None, "fft"),
            P("band", None, "fft"),
        ),
        out_specs=(P("band", None, "fft"), P(None, "fft", "band")),
        check_vma=False,
    )
```

time: 69.9 us -> 52.9 us (0.76)
  Pallas kernels: 62.2 us -> 50 us
  local copies, waits for them, and re-layouts: 6.09 us -> 2.08 us
  other arithmetic: 0.8 us -> 0 us
    pallas_call x1, Pallas kernels: 62.2 us -> 50 us  [per_device(): pl.pallas_call(functools.partial(kernel, dims), out_shape=[jax.ShapeDtype...]
    reshape x5 -> x0, local copies, waits for them, and re-layouts: 5.42 us -> none  [the longest x1 1.54 us: per_device(): orbitals.reshape(parts, waves)]
    unnamed x4, local copies, waits for them, and re-layouts: 0.67 us -> 2.08 us
where the time goes in v1:
time: 52.9 us; the launch traced here: 52.8 us
  Pallas kernels  50 us (95%)
  local copies, waits for them, and re-layouts  2.08 us (4%)
  between operations  0.65 us (1%)
    pallas_call x1, Pallas kernels, per_device(): pl.pallas_call(functools.partial(kernel, dims), out_shape=[jax.ShapeDtype...  50 us
    unnamed x4, local copies, waits for them, and re-layouts  2.08 us

profile of v1, /device:TPU:8, one launch (start us, length us, event | category | flops | bytes accessed | tf_op | source)
XLA Modules:
  0.0 52.8 jit_solution(11605558946555441424)
XLA Ops:
  0.6 50.0 %apply.1 = (bf16[4,2,4096]{2,1,0:T(2,128)(2,1)}, f32[2,1,4]{2,1,0:T(1,128)}) custom-call(bf16[4,2,4096]{2,1,0:T(2,128)(2,1)} %refs_0_.1, s32[1,4096]{1,0:T(1,128)} %bitcast.2, s32[1,128]{1,0:T(1,128)} %bitcast.3, f32[3,192,192]{2,1,0:T(8,128)} %refs_3_.1, bf16[16,2,4096]{2,1,0:T(2,128)(2,1)} %refs_4_.1, bf16[4,2,4096]{2,1,0:T(2,128)(2,1)} %refs_5_.1, ...), custom_call_target="tpu_custom_call" | custom-call | tf_op jit(solution)/shard_map/apply/pallas_call | solution.py:409
  50.7 0.0 copy-start
  50.7 1.5 %copy.22 = bf16[4,2,4096]{2,1,0:T(2,128)(2,1)} copy(bf16[4,2,4096]{2,1,0:T(2,128)(2,1)} %get-tuple-element.4) | data formatting | bytes 131072
  52.2 0.0 copy-done
  52.2 0.6 %copy.23 = f32[2,1,4]{2,1,0:T(1,128)} copy(f32[2,1,4]{2,1,0:T(1,128)S(1)} %copy-done) | data formatting | bytes 64
Async XLA Ops:
  50.7 1.5 %copy-start = (f32[2,1,4]{2,1,0:T(1,128)S(1)}, f32[2,1,4]{2,1,0:T(1,128)}, u32[]{:S(2)}) copy-start(f32[2,1,4]{2,1,0:T(1,128)} %get-tuple-element.5) | copy-start | bytes 100

commit v2 on v1

--- a/solution.py
+++ b/solution.py
@@ -72,9 +72,13 @@
     return pl.BlockSpec(memory_space=pltpu.VMEM)
 
 
-def hot(rows, index, kind=BF16):
+def hot(count, index, numbers):
     lanes = index.shape[1]
-    return (lax.broadcasted_iota(jnp.int32, (rows, lanes), 0) == index).astype(F32).astype(kind)
+    index = jnp.broadcast_to(index.astype(F32), (16, lanes)).astype(BF16)
+    rows = numbers[:count].reshape(count // 16, 16, numbers.shape[1])
+    rows = jnp.concatenate([rows] * (lanes // numbers.shape[1]), axis=2)
+    one, zero = jnp.ones((), BF16), jnp.zeros((), BF16)
+    return jnp.where(rows == index[None], one, zero).reshape(count, lanes)
 
 
 def frequency(values, grid):
@@ -98,22 +102,30 @@
 
 def others(axis, count, act):
     me = lax.axis_index(axis)
+    skip = count // 2 + count // 8 + 1
 
     def step(j, carry):
-        act(me, lax.rem(me + j, count))
+        act(me, lax.rem(me + skip * j, count))
         return carry
 
     lax.fori_loop(1, count, step, 0, unroll=3)
+
+
+def near(step):
+    return lax.rem(lax.div(step * (step + 1), 2), 4)
 
 
 def kernel(dims, *refs):
     owners, groups, grid, depth, sticks, waves, bands, teams, subs = dims
-    orb, slot, column, pot, sub, prev = refs[:6]
-    zf, zb, yf, xf, xb, yb = (refs[6 + 2 * i : 8 + 2 * i] for i in range(6))
-    out, inter = refs[18:20]
+    inputs, (out, inter), refs = refs[:18], refs[18:20], refs[20:]
+    prev = inputs[5]
+    held, refs = refs[:17], refs[17:]
+    orb, slot, column, pot, sub = held[:5]
+    zf, zb, yf, xf, xb, yb = (held[5 + 2 * i : 7 + 2 * i] for i in range(6))
     (high_hot, low_hot, rep, stage, send, recv, send2, recv2, cols, ymask, ymask_t, xmask,
-     val, gre, gim, back, pots, turn, pall, r1, r2, r3) = refs[20:42]
-    col_s, col_r, fwd_s, fwd_r, bwd_s, bwd_r, prev_s, prev_r, one_s, one_r, two_s, two_r = refs[42:]
+     val, gre, gim, back, pots, turn, left, numbers, pall, r1, r2, r3) = refs[:24]
+    (in_s, col_s, col_r, fwd_s, first_r, fwd_r, bwd_s, bwd_r, prev_s, prev_r,
+     one_s, one_r, two_s, two_r) = refs[24:]
     parts = 2 * bands
     wide = 4 * sticks
     half = grid // 2
@@ -123,6 +135,9 @@
     chunk = 512
     me = lax.axis_index("fft")
     team = lax.axis_index("band")
+    batch = lax.div(lax.rem(me, 16), 4)
+    within = 4 * lax.div(me, 16) + lax.rem(me, 4)
+    place = 16 * batch + within
 
     barrier = pltpu.get_barrier_semaphore()
 
@@ -134,28 +149,31 @@
 
         return act
 
+    given = [*inputs[:5], *inputs[6:]]
+    fetches = [
+        pltpu.make_async_copy(src, dst, in_s.at[i])
+        for i, (src, dst) in enumerate(zip(given, held, strict=True))
+    ]
+    for i in (1, 0, 2, 5, 6):
+        fetches[i].start()
     others("fft", owners, greet("fft"))
     others("band", teams, greet("band"))
+    for i in (3, 4, *range(7, 17)):
+        fetches[i].start()
 
     with jax.named_scope("hots"):
+        numbers[...] = lax.broadcasted_iota(jnp.int32, (256, 128), 0).astype(F32).astype(BF16)
+        for i in (0, 1, 2):
+            fetches[i].wait()
         for c in range(0, waves, chunk):
             cut = slice(c, c + chunk)
             sl = slot[:, cut]
-            high_hot[:, cut] = hot(half, lax.div(sl, low))
-            low_hot[:, cut] = hot(low, lax.rem(sl, low))
+            high_hot[:, cut] = hot(half, lax.div(sl, low), numbers[...])
+            low_hot[:, cut] = hot(low, lax.rem(sl, low), numbers[...])
             for b in range(bands):
                 pair = orb[b, :, cut].astype(F32)
                 for p in range(2):
                     rep[2 * b + p, :, cut] = jnp.broadcast_to(pair[p : p + 1], (16, chunk)).astype(BF16)
-
-    with jax.named_scope("barrier"):
-        pl.semaphore_wait(barrier, owners + teams - 2)
-        others("fft", owners, lambda own, peer: start_to(
-            column, cols.at[own], col_s, col_r, "fft", peer))
-        pltpu.make_async_copy(column, cols.at[me], col_r).start()
-        others("band", teams, lambda own, peer: start_to(
-            prev, pall.at[own], prev_s, prev_r, "band", peer))
-        pltpu.make_async_copy(prev, pall.at[team], prev_r).start()
 
     with jax.named_scope("zdft"):
         got = None
@@ -168,6 +186,8 @@
             piece = dot_nt(block, low_hot[:, cut])
             got = piece if got is None else got + piece
         got = got.astype(BF16)
+        for i in (5, 6):
+            fetches[i].wait()
         for b in range(bands):
             cut = got[2 * b * half : 2 * (b + 1) * half]
             field = jnp.concatenate(
@@ -182,29 +202,10 @@
         for z in range(depth):
             for f in range(owners):
                 send[z, f] = stage[z, parts * f : parts * (f + 1), :].astype(BF16)
-    with jax.named_scope("sends"):
-        for z in range(depth):
-            others("fft", owners, lambda own, peer, z=z: start_to(
-                send.at[z, peer], recv.at[z, own], fwd_s.at[z], fwd_r.at[z], "fft", peer))
-            pltpu.make_async_copy(send.at[z, me], recv.at[z, me], fwd_r.at[z]).start()
-
-    with jax.named_scope("masks"):
-        wait_bytes(cols, col_r)
-        for g in range(groups):
-            for d in range(4):
-                col = cols[4 * g + d]
-                x = lax.div(col, grid)
-                y = col - x * grid
-                x = x - 4 * depth * g
-                y = jnp.where(y >= half, y + (128 - half), y)
-                lanes = slice(sticks * d, sticks * (d + 1))
-                ymask[g, :, lanes] = hot(256, y)
-                xmask[g, :, lanes] = hot(16, x, F32)
-                yt = jnp.broadcast_to(y.astype(F32), (sticks, sticks)).T.astype(jnp.int32)
-                wide_y = jnp.concatenate([yt, yt], axis=1)
-                ymask_t[g, lanes, :] = (
-                    lax.broadcasted_iota(jnp.int32, (sticks, 256), 1) == wide_y
-                ).astype(F32).astype(BF16)
+
+    with jax.named_scope("early"):
+        for i in (3, 4, *range(7, 17)):
+            fetches[i].wait()
         side = jnp.zeros((grid, 256 - grid), F32)
         gap = jnp.zeros((128 - half, 256), F32)
 
@@ -221,76 +222,57 @@
             table = jnp.concatenate([even, odd], axis=0).T[:grid]
             even, odd = sorted_rows(jnp.concatenate([table, side], axis=1))
             pots[z] = jnp.concatenate([even, gap, odd, gap], axis=0).T[:grid]
-
-    with jax.named_scope("inter1"):
-        wait_bytes(pall, prev_r)
-        left = jnp.concatenate([sub[j] for j in range(subs)], axis=0)
-        for t in range(teams):
-            right = jnp.concatenate(
-                [pall[t, i][p : p + 1] for p in range(2) for i in range(bands)], axis=0
-            )
-            part = dot_nt(left, right)
-            part = jnp.concatenate([part, jnp.zeros((2 * subs, 128 - parts), F32)], axis=1)
-            for j in range(subs):
-                r1[t, j] = part[2 * j : 2 * j + 2, :]
+        left[...] = jnp.concatenate([sub[j] for j in range(subs)], axis=0)
+
+    with jax.named_scope("barrier"):
+        pl.semaphore_wait(barrier, owners + teams - 2)
+    with jax.named_scope("sends"):
+        others("fft", owners, lambda own, peer: start_to(
+            column, cols.at[place], col_s, col_r.at[batch], "fft", peer))
+        pltpu.make_async_copy(column, cols.at[place], col_r.at[batch]).start()
+        others("fft", owners, lambda own, peer: start_to(
+            send.at[0, peer], recv.at[0, place], fwd_s.at[0], first_r.at[batch], "fft", peer))
+        pltpu.make_async_copy(send.at[0, me], recv.at[0, place], first_r.at[batch]).start()
+        for z in range(1, depth):
+            others("fft", owners, lambda own, peer, z=z: start_to(
+                send.at[z, peer], recv.at[z, place], fwd_s.at[z], fwd_r.at[z], "fft", peer))
+            pltpu.make_async_copy(send.at[z, me], recv.at[z, place], fwd_r.at[z]).start()
         others("band", teams, lambda own, peer: start_to(
-            r1.at[peer], r2.at[own], one_s, one_r, "band", peer))
-        pltpu.make_async_copy(r1.at[team], r2.at[team], one_r).start()
-
-    def plane(z, carry):
-        with jax.named_scope("waitz"):
-            wait_bytes(recv.at[z], fwd_r.at[z])
-
-        def scatter(g, carry):
-            for d in range(4):
-                val[g, :, sticks * d : sticks * (d + 1)] = recv[z, 4 * g + d].astype(F32)
-            mask = xmask[g]
-            block = jnp.concatenate(
-                [(mask * val[g, r : r + 1, :]).astype(BF16) for r in range(parts)], axis=0
-            )
-            got = dot(block, ymask_t[g]).astype(BF16)
-            at = pl.ds(pl.multiple_of(16 * g, 16), 16)
-            gre[:, at, :] = got[: bands * 16].reshape(bands, 16, 256)
-            gim[:, at, :] = got[bands * 16 :].reshape(bands, 16, 256)
-            return carry
-
-        with jax.named_scope("scatter"):
-            lax.fori_loop(0, groups, scatter, 0, unroll=4)
-
-        with jax.named_scope("local"):
-            local(z)
-
-        def quarter(i, carry):
-            q = lax.rem(lax.div(me, 16) + i, owners // 16)
-            for k in range(4):
-                g = 4 * q + k
-                at = pl.ds(pl.multiple_of(16 * g, 16), 16)
-                block = back[:, at, :].reshape(parts * 16, 256)
-                t = dot(block, ymask[g]).reshape(parts, 16, wide)
-                got = jnp.sum(t * xmask[g][None], axis=1)
-                for d in range(4):
-                    send2[z, 4 * g + d] = got[:, sticks * d : sticks * (d + 1)].astype(BF16)
-
-            def give(j, carry):
-                peer = 16 * q + lax.rem(me + j, 16)
-                start_to(send2.at[z, peer], recv2.at[z, me], bwd_s.at[z], bwd_r.at[z], "fft", peer)
-                return carry
-
-            lax.fori_loop(1, 16, give, 0, unroll=5)
-
-            @pl.when(i > 0)
-            def _():
-                give(0, 0)
-
-            @pl.when(i == 0)
-            def _():
-                pltpu.make_async_copy(send2.at[z, me], recv2.at[z, me], bwd_r.at[z]).start()
-
-            return carry
-
-        with jax.named_scope("pick"):
-            lax.fori_loop(0, owners // 16, quarter, 0)
-        return carry
+            prev, pall.at[own], prev_s, prev_r, "band", peer))
+        pltpu.make_async_copy(prev, pall.at[team], prev_r).start()
+
+    def masks(h):
+        g = 4 * lax.rem(h, 4) + lax.div(h, 4)
+        for d in range(4):
+            col = cols[4 * h + d]
+            x = lax.div(col, grid)
+            y = col - x * grid
+            x = x - 4 * depth * g
+            y = jnp.where(y >= half, y + (128 - half), y)
+            lanes = slice(sticks * d, sticks * (d + 1))
+            ymask[h, :, lanes] = hot(256, y, numbers[...])
+            xmask[h, :, lanes] = hot(16, x, numbers[...])
+            yt = jnp.broadcast_to(y.astype(F32), (sticks, sticks)).T.astype(BF16)
+            line = lax.broadcasted_iota(jnp.int32, (16, 128), 1).astype(F32)
+            one, zero = jnp.ones((), BF16), jnp.zeros((), BF16)
+            for q in range(2):
+                at = (line + 128.0 * q).astype(BF16)[None]
+                same = yt.reshape(sticks // 16, 16, 128) == at
+                ymask_t[h, lanes, 128 * q : 128 * (q + 1)] = jnp.where(same, one, zero).reshape(sticks, 128)
+
+    def scatter(z, h):
+        for d in range(4):
+            val[h, :, sticks * d : sticks * (d + 1)] = recv[z, 4 * h + d].astype(F32)
+        mask = xmask[h]
+        block = jnp.concatenate(
+            [mask * jnp.broadcast_to(val[h, r : r + 1, :], (16, wide)).astype(BF16)
+             for r in range(parts)], axis=0
+        )
+        got = dot(block, ymask_t[h]).astype(BF16)
+        g = 4 * lax.rem(h, 4) + lax.div(h, 4)
+        at = pl.ds(pl.multiple_of(16 * g, 16), 16)
+        gre[:, at, :] = got[: bands * 16].reshape(bands, 16, 256)
+        gim[:, at, :] = got[bands * 16 :].reshape(bands, 16, 256)
 
     def local(z):
         ve, vo = pots[z, :half], pots[z, half:]
@@ -325,6 +307,96 @@
             p, m = (e + o).astype(BF16), (e - o).astype(BF16)
             back[b] = jnp.concatenate([p[:, :128], m[:, :128]], axis=1)
             back[bands + b] = jnp.concatenate([p[:, 128:], m[:, 128:]], axis=1)
+
+    def quarter(z, i):
+        q = lax.rem(batch + near(3 - i), 4)
+        line = lax.broadcasted_iota(jnp.int32, (16, parts * 16), 1)
+        row = lax.broadcasted_iota(jnp.int32, (16, parts * 16), 0)
+        ones = (lax.div(line, 16) == row).astype(F32).astype(BF16)
+        for k in range(4):
+            h = 4 * q + k
+            g = 4 * k + q
+            at = pl.ds(pl.multiple_of(16 * g, 16), 16)
+            block = back[:, at, :].reshape(parts * 16, 256)
+            t = dot(block, ymask[h]).astype(BF16).reshape(parts, 16, wide)
+            t = (t * xmask[h][None]).reshape(parts * 16, wide)
+            got = dot(ones, t)[:parts]
+            for d in range(4):
+                send2[z, 4 * h + d] = got[:, sticks * d : sticks * (d + 1)].astype(BF16)
+
+        def give(j, carry):
+            t = lax.rem(within + 9 * j, 16)
+            peer = 16 * lax.div(t, 4) + 4 * q + lax.rem(t, 4)
+            start_to(send2.at[z, 16 * q + t], recv2.at[z, me], bwd_s.at[z], bwd_r.at[z], "fft", peer)
+            return carry
+
+        lax.fori_loop(1, 16, give, 0, unroll=5)
+
+        @pl.when(i < 3)
+        def _():
+            give(0, 0)
+
+        @pl.when(i == 3)
+        def _():
+            pltpu.make_async_copy(send2.at[z, place], recv2.at[z, me], bwd_r.at[z]).start()
+
+    def work(z):
+        with jax.named_scope("local"):
+            local(z)
+
+        def step(i, carry):
+            quarter(z, i)
+            return carry
+
+        with jax.named_scope("pick"):
+            lax.fori_loop(0, 4, step, 0)
+
+    def first(i, carry):
+        q = lax.rem(batch + near(i), 4)
+        wait_bytes(cols.at[pl.ds(16 * q, 16)], col_r.at[q])
+        for k in range(4):
+            masks(4 * q + k)
+        wait_bytes(recv.at[0, pl.ds(16 * q, 16)], first_r.at[q])
+        for k in range(4):
+            scatter(0, 4 * q + k)
+        return carry
+
+    with jax.named_scope("first"):
+        lax.fori_loop(0, 4, first, 0)
+
+    def plane(z, carry):
+        @pl.when(z > 0)
+        def _():
+            wait_bytes(recv.at[z], fwd_r.at[z])
+
+            def step(h, carry):
+                scatter(z, h)
+                return carry
+
+            with jax.named_scope("scatter"):
+                lax.fori_loop(0, groups, step, 0, unroll=8)
+
+        work(z)
+
+        @pl.when(z == 0)
+        def _():
+            with jax.named_scope("inter1"):
+                wait_bytes(pall, prev_r)
+                for t in range(teams):
+                    right = jnp.concatenate(
+                        [pall[t, i][p : p + 1] for p in range(2) for i in range(bands)], axis=0
+                    )
+                    part = dot_nt(left[...], right)
+                    part = jnp.concatenate(
+                        [part, jnp.zeros((2 * subs, 128 - parts), F32)], axis=1
+                    )
+                    for j in range(subs):
+                        r1[t, j] = part[2 * j : 2 * j + 2, :]
+                others("band", teams, lambda own, peer: start_to(
+                    r1.at[peer], r2.at[own], one_s, one_r, "band", peer))
+                pltpu.make_async_copy(r1.at[team], r2.at[team], one_r).start()
+
+        return carry
 
     lax.fori_loop(0, depth, plane, 0)
 
@@ -401,10 +473,20 @@
     parts = 2 * bands
     half = grid // 2
     every = tables(grid, owners)
+    given = [
+        orbitals,
+        sphere_slot.reshape(1, waves),
+        stick_column.reshape(1, sticks),
+        potential,
+        subspace,
+        previous,
+        *every,
+    ]
     dims = (owners, groups, grid, depth, sticks, waves, bands, teams, subs)
     message = pltpu.VMEM((depth, owners, parts, sticks), BF16)
     sums = pltpu.VMEM((teams, subs, 2, 128), F32)
     one = pltpu.SemaphoreType.DMA
+    four = pltpu.SemaphoreType.DMA((4,))
     several = pltpu.SemaphoreType.DMA((depth,))
     return tuple(pl.pallas_call(
         functools.partial(kernel, dims),
@@ -412,9 +494,10 @@
             jax.ShapeDtypeStruct(orbitals.shape, BF16),
             jax.ShapeDtypeStruct((2, 1, bands), F32),
         ],
-        in_specs=[vmem() for _ in range(6 + len(every))],
+        in_specs=[pl.BlockSpec(memory_space=pl.ANY) for _ in range(6 + len(every))],
         out_specs=[vmem(), vmem()],
         scratch_shapes=[
+            *[pltpu.VMEM(t.shape, t.dtype) for t in given if t is not previous],
             pltpu.VMEM((half, waves), BF16),
             pltpu.VMEM((2 * sticks, waves), BF16),
             pltpu.VMEM((parts, 16, waves), BF16),
@@ -426,32 +509,27 @@
             pltpu.VMEM((owners, 1, sticks), jnp.int32),
             pltpu.VMEM((groups, 256, 4 * sticks), BF16),
             pltpu.VMEM((groups, 4 * sticks, 256), BF16),
-            pltpu.VMEM((groups, 16, 4 * sticks), F32),
+            pltpu.VMEM((groups, 16, 4 * sticks), BF16),
             pltpu.VMEM((groups, parts, 4 * sticks), F32),
             pltpu.VMEM((bands, groups * 16, 256), BF16),
             pltpu.VMEM((bands, groups * 16, 256), BF16),
             pltpu.VMEM((parts, groups * 16, 256), BF16),
             pltpu.VMEM((depth, grid, 256), F32),
             pltpu.VMEM((2, grid, 128), F32),
+            pltpu.VMEM((2 * subs, waves), BF16),
+            pltpu.VMEM((256, 128), BF16),
             pltpu.VMEM((teams, *previous.shape), BF16),
             sums,
             sums,
             pltpu.VMEM((owners, 2, 128), F32),
-            one, one, several, several, several, several, one, one, one, one, one, one,
+            pltpu.SemaphoreType.DMA((17,)),
+            one, four, several, four, several, several, several, one, one, one, one, one, one,
         ],
         compiler_params=pltpu.CompilerParams(
             vmem_limit_bytes=60 * 2**20, collective_id=0, has_side_effects=True
         ),
         name="apply",
-    )(
-        orbitals,
-        sphere_slot.reshape(1, waves),
-        stick_column.reshape(1, sticks),
-        potential,
-        subspace,
-        previous,
-        *every,
-    ))
+    )(*given))
 
 
 def solution(mesh):

time: 52.9 us -> 54.3 us (1.026)
  Pallas kernels: 50 us -> 51.3 us
    pallas_call x1, Pallas kernels: 50 us -> 51.3 us  [per_device(): pl.pallas_call(functools.partial(kernel, dims), out_shape=[jax.ShapeDtype...]
where the time goes in v2:
time: 54.3 us; the launch traced here: 54 us
  Pallas kernels  51.3 us (94%)
  local copies, waits for them, and re-layouts  2.08 us (4%)
  between operations  0.65 us (1%)
    pallas_call x1, Pallas kernels, per_device(): pl.pallas_call(functools.partial(kernel, dims), out_shape=[jax.ShapeDtype...  51.3 us
    unnamed x4, local copies, waits for them, and re-layouts  2.08 us

profile of v2, /device:TPU:8, one launch (start us, length us, event | category | flops | bytes accessed | tf_op | source)
XLA Modules:
  0.0 54.0 jit_solution(6454752817523056492)
XLA Ops:
  0.6 51.3 %apply.1 = (bf16[4,2,4096]{2,1,0:T(2,128)(2,1)}, f32[2,1,4]{2,1,0:T(1,128)}) custom-call(bf16[4,2,4096]{2,1,0:T(2,128)(2,1)} %refs_0_.1, s32[1,4096]{1,0:T(1,128)} %bitcast.2, s32[1,128]{1,0:T(1,128)} %bitcast.3, f32[3,192,192]{2,1,0:T(8,128)} %refs_3_.1, bf16[16,2,4096]{2,1,0:T(2,128)(2,1)} %refs_4_.1, bf16[4,2,4096]{2,1,0:T(2,128)(2,1)} %refs_5_.1, ...), custom_call_target="tpu_custom_call" | custom-call | tf_op jit(solution)/shard_map/apply/pallas_call | solution.py:491
  51.9 0.0 copy-start
  51.9 1.5 %copy.22 = bf16[4,2,4096]{2,1,0:T(2,128)(2,1)} copy(bf16[4,2,4096]{2,1,0:T(2,128)(2,1)} %get-tuple-element.4) | data formatting | bytes 131072
  53.4 0.0 copy-done
  53.4 0.6 %copy.23 = f32[2,1,4]{2,1,0:T(1,128)} copy(f32[2,1,4]{2,1,0:T(1,128)S(1)} %copy-done) | data formatting | bytes 64
Async XLA Ops:
  51.9 1.5 %copy-start = (f32[2,1,4]{2,1,0:T(1,128)S(1)}, f32[2,1,4]{2,1,0:T(1,128)}, u32[]{:S(2)}) copy-start(f32[2,1,4]{2,1,0:T(1,128)} %get-tuple-element.5) | copy-start | bytes 100

commit v3 on v2

--- a/solution.py
+++ b/solution.py
@@ -100,15 +100,22 @@
     pltpu.make_async_copy(ref, ref, sem).wait()
 
 
-def others(axis, count, act):
-    me = lax.axis_index(axis)
-    skip = count // 2 + count // 8 + 1
-
-    def step(j, carry):
-        act(me, lax.rem(me + skip * j, count))
-        return carry
-
-    lax.fori_loop(1, count, step, 0, unroll=3)
+def hops(step):
+    across, along, over = step
+    return min(across, 4 - across) + min(along, 8 - along) + 2 * over
+
+
+def peers_of(me):
+    steps = [(i, j, k) for i in range(4) for j in range(8) for k in range(2)]
+    steps = sorted(steps[1:], key=hops, reverse=True)
+    across = [16 * lax.rem(lax.div(me, 16) + i, 4) for i in range(4)]
+    along = [2 * lax.rem(lax.div(me, 2) + j, 8) for j in range(8)]
+    over = [lax.rem(me + k, 2) for k in range(2)]
+    return [across[i] + along[j] + over[k] for i, j, k in steps]
+
+
+def mates_of(team, teams):
+    return [lax.rem(team + j, teams) for j in range(1, teams)]
 
 
 def near(step):
@@ -139,25 +146,26 @@
     within = 4 * lax.div(me, 16) + lax.rem(me, 4)
     place = 16 * batch + within
 
+    peers, mates = peers_of(me), mates_of(team, teams)
+
     barrier = pltpu.get_barrier_semaphore()
 
-    def greet(axis):
-        def act(own, peer):
-            pl.semaphore_signal(
-                barrier, inc=1, device_id={axis: peer}, device_id_type=pl.DeviceIdType.MESH
-            )
-
-        return act
+    def greet(axis, peer):
+        pl.semaphore_signal(
+            barrier, inc=1, device_id={axis: peer}, device_id_type=pl.DeviceIdType.MESH
+        )
 
     given = [*inputs[:5], *inputs[6:]]
     fetches = [
         pltpu.make_async_copy(src, dst, in_s.at[i])
         for i, (src, dst) in enumerate(zip(given, held, strict=True))
     ]
+    for peer in peers:
+        greet("fft", peer)
     for i in (1, 0, 2, 5, 6):
         fetches[i].start()
-    others("fft", owners, greet("fft"))
-    others("band", teams, greet("band"))
+    for mate in mates:
+        greet("band", mate)
     for i in (3, 4, *range(7, 17)):
         fetches[i].start()
 
@@ -203,6 +211,23 @@
             for f in range(owners):
                 send[z, f] = stage[z, parts * f : parts * (f + 1), :].astype(BF16)
 
+    with jax.named_scope("barrier"):
+        pl.semaphore_wait(barrier, owners + teams - 2)
+    with jax.named_scope("sends"):
+        for peer in peers:
+            start_to(column, cols.at[place], col_s, col_r.at[batch], "fft", peer)
+        pltpu.make_async_copy(column, cols.at[place], col_r.at[batch]).start()
+        for peer in peers:
+            start_to(send.at[0, peer], recv.at[0, place], fwd_s.at[0], first_r.at[batch], "fft", peer)
+        pltpu.make_async_copy(send.at[0, me], recv.at[0, place], first_r.at[batch]).start()
+        for mate in mates:
+            start_to(prev, pall.at[team], prev_s, prev_r, "band", mate)
+        pltpu.make_async_copy(prev, pall.at[team], prev_r).start()
+        for z in range(1, depth):
+            for peer in peers:
+                start_to(send.at[z, peer], recv.at[z, place], fwd_s.at[z], fwd_r.at[z], "fft", peer)
+            pltpu.make_async_copy(send.at[z, me], recv.at[z, place], fwd_r.at[z]).start()
+
     with jax.named_scope("early"):
         for i in (3, 4, *range(7, 17)):
             fetches[i].wait()
@@ -223,23 +248,6 @@
             even, odd = sorted_rows(jnp.concatenate([table, side], axis=1))
             pots[z] = jnp.concatenate([even, gap, odd, gap], axis=0).T[:grid]
         left[...] = jnp.concatenate([sub[j] for j in range(subs)], axis=0)
-
-    with jax.named_scope("barrier"):
-        pl.semaphore_wait(barrier, owners + teams - 2)
-    with jax.named_scope("sends"):
-        others("fft", owners, lambda own, peer: start_to(
-            column, cols.at[place], col_s, col_r.at[batch], "fft", peer))
-        pltpu.make_async_copy(column, cols.at[place], col_r.at[batch]).start()
-        others("fft", owners, lambda own, peer: start_to(
-            send.at[0, peer], recv.at[0, place], fwd_s.at[0], first_r.at[batch], "fft", peer))
-        pltpu.make_async_copy(send.at[0, me], recv.at[0, place], first_r.at[batch]).start()
-        for z in range(1, depth):
-            others("fft", owners, lambda own, peer, z=z: start_to(
-                send.at[z, peer], recv.at[z, place], fwd_s.at[z], fwd_r.at[z], "fft", peer))
-            pltpu.make_async_copy(send.at[z, me], recv.at[z, place], fwd_r.at[z]).start()
-        others("band", teams, lambda own, peer: start_to(
-            prev, pall.at[own], prev_s, prev_r, "band", peer))
-        pltpu.make_async_copy(prev, pall.at[team], prev_r).start()
 
     def masks(h):
         g = 4 * lax.rem(h, 4) + lax.div(h, 4)
@@ -308,50 +316,66 @@
             back[b] = jnp.concatenate([p[:, :128], m[:, :128]], axis=1)
             back[bands + b] = jnp.concatenate([p[:, 128:], m[:, 128:]], axis=1)
 
-    def quarter(z, i):
-        q = lax.rem(batch + near(3 - i), 4)
+    around = [lax.rem(batch + o, 4) for o in range(4)]
+    across = [lax.rem(lax.div(me, 16) + o, 4) for o in range(4)]
+    inside = [lax.rem(lax.rem(me, 4) + o, 4) for o in range(4)]
+
+    def section(z, turns):
         line = lax.broadcasted_iota(jnp.int32, (16, parts * 16), 1)
         row = lax.broadcasted_iota(jnp.int32, (16, parts * 16), 0)
         ones = (lax.div(line, 16) == row).astype(F32).astype(BF16)
-        for k in range(4):
-            h = 4 * q + k
-            g = 4 * k + q
+        spots = [(4 * around[o] + k, 4 * k + around[o]) for o in turns for k in range(4)]
+        tall = []
+        for h, g in spots:
             at = pl.ds(pl.multiple_of(16 * g, 16), 16)
-            block = back[:, at, :].reshape(parts * 16, 256)
-            t = dot(block, ymask[h]).astype(BF16).reshape(parts, 16, wide)
-            t = (t * xmask[h][None]).reshape(parts * 16, wide)
+            tall.append(dot(back[:, at, :].reshape(parts * 16, 256), ymask[h]))
+        cut = []
+        for t, (h, g) in zip(tall, spots, strict=True):
+            t = t.astype(BF16).reshape(parts, 16, wide) * xmask[h][None]
+            cut.append(t.reshape(parts * 16, wide))
+        for t, (h, g) in zip(cut, spots, strict=True):
             got = dot(ones, t)[:parts]
             for d in range(4):
                 send2[z, 4 * h + d] = got[:, sticks * d : sticks * (d + 1)].astype(BF16)
-
-        def give(j, carry):
-            t = lax.rem(within + 9 * j, 16)
-            peer = 16 * lax.div(t, 4) + 4 * q + lax.rem(t, 4)
-            start_to(send2.at[z, 16 * q + t], recv2.at[z, me], bwd_s.at[z], bwd_r.at[z], "fft", peer)
-            return carry
-
-        lax.fori_loop(1, 16, give, 0, unroll=5)
-
-        @pl.when(i < 3)
-        def _():
-            give(0, 0)
-
-        @pl.when(i == 3)
-        def _():
-            pltpu.make_async_copy(send2.at[z, place], recv2.at[z, me], bwd_r.at[z]).start()
+        for o in turns:
+            for y in (2, 1, 3, 0):
+                for r in (2, 1, 3, 0):
+                    spot = 16 * around[o] + 4 * across[y] + inside[r]
+                    peer = 16 * across[y] + 4 * around[o] + inside[r]
+                    if o or y or r:
+                        start_to(send2.at[z, spot], recv2.at[z, me], bwd_s.at[z], bwd_r.at[z], "fft", peer)
+                    else:
+                        pltpu.make_async_copy(send2.at[z, spot], recv2.at[z, me], bwd_r.at[z]).start()
 
     def work(z):
         with jax.named_scope("local"):
             local(z)
 
-        def step(i, carry):
-            quarter(z, i)
-            return carry
-
         with jax.named_scope("pick"):
-            lax.fori_loop(0, 4, step, 0)
+            section(z, (2, 3))
+            section(z, (1, 0))
+
+    def overlaps():
+        wait_bytes(pall, prev_r)
+        for t in range(teams):
+            right = jnp.concatenate(
+                [pall[t, i][p : p + 1] for p in range(2) for i in range(bands)], axis=0
+            )
+            part = dot_nt(left[...], right)
+            part = jnp.concatenate(
+                [part, jnp.zeros((2 * subs, 128 - parts), F32)], axis=1
+            )
+            for j in range(subs):
+                r1[t, j] = part[2 * j : 2 * j + 2, :]
+        for mate in mates:
+            start_to(r1.at[mate], r2.at[team], one_s, one_r, "band", mate)
+        pltpu.make_async_copy(r1.at[team], r2.at[team], one_r).start()
 
     def first(i, carry):
+        @pl.when(i == 3)
+        def _():
+            overlaps()
+
         q = lax.rem(batch + near(i), 4)
         wait_bytes(cols.at[pl.ds(16 * q, 16)], col_r.at[q])
         for k in range(4):
@@ -378,32 +402,16 @@
 
         work(z)
 
-        @pl.when(z == 0)
-        def _():
-            with jax.named_scope("inter1"):
-                wait_bytes(pall, prev_r)
-                for t in range(teams):
-                    right = jnp.concatenate(
-                        [pall[t, i][p : p + 1] for p in range(2) for i in range(bands)], axis=0
-                    )
-                    part = dot_nt(left[...], right)
-                    part = jnp.concatenate(
-                        [part, jnp.zeros((2 * subs, 128 - parts), F32)], axis=1
-                    )
-                    for j in range(subs):
-                        r1[t, j] = part[2 * j : 2 * j + 2, :]
-                others("band", teams, lambda own, peer: start_to(
-                    r1.at[peer], r2.at[own], one_s, one_r, "band", peer))
-                pltpu.make_async_copy(r1.at[team], r2.at[team], one_r).start()
-
         return carry
 
     lax.fori_loop(0, depth, plane, 0)
 
     with jax.named_scope("inter2"):
         wait_bytes(r2, one_r)
-        others("fft", owners, lambda own, peer: start_to(
-            r2.at[lax.div(peer, subs), lax.rem(peer, subs)], r3.at[own], two_s, two_r, "fft", peer))
+        for peer in peers:
+            start_to(
+                r2.at[lax.div(peer, subs), lax.rem(peer, subs)], r3.at[me], two_s, two_r, "fft", peer
+            )
         pltpu.make_async_copy(
             r2.at[lax.div(me, subs), lax.rem(me, subs)], r3.at[me], two_r).start()
 

time: 54.3 us -> 45.1 us (0.83)
  Pallas kernels: 51.3 us -> 41.7 us
    pallas_call x1, Pallas kernels: 51.3 us -> 41.7 us  [per_device(): pl.pallas_call(functools.partial(kernel, dims), out_shape=[jax.ShapeDtype...]
where the time goes in v3:
time: 45.1 us; the launch traced here: 44.4 us
  Pallas kernels  41.7 us (92%)
  local copies, waits for them, and re-layouts  2.08 us (5%)
  between operations  0.65 us (1%)
    pallas_call x1, Pallas kernels, per_device(): pl.pallas_call(functools.partial(kernel, dims), out_shape=[jax.ShapeDtype...  41.7 us
    unnamed x4, local copies, waits for them, and re-layouts  2.08 us

profile of v3, /device:TPU:8, one launch (start us, length us, event | category | flops | bytes accessed | tf_op | source)
XLA Modules:
  0.0 44.4 jit_solution(1375736964254698972)
XLA Ops:
  0.6 41.7 %apply.1 = (bf16[4,2,4096]{2,1,0:T(2,128)(2,1)}, f32[2,1,4]{2,1,0:T(1,128)}) custom-call(bf16[4,2,4096]{2,1,0:T(2,128)(2,1)} %refs_0_.1, s32[1,4096]{1,0:T(1,128)} %bitcast.2, s32[1,128]{1,0:T(1,128)} %bitcast.3, f32[3,192,192]{2,1,0:T(8,128)} %refs_3_.1, bf16[16,2,4096]{2,1,0:T(2,128)(2,1)} %refs_4_.1, bf16[4,2,4096]{2,1,0:T(2,128)(2,1)} %refs_5_.1, ...), custom_call_target="tpu_custom_call" | custom-call | tf_op jit(solution)/shard_map/apply/pallas_call | solution.py:499
  42.3 0.0 copy-start
  42.3 1.5 %copy.22 = bf16[4,2,4096]{2,1,0:T(2,128)(2,1)} copy(bf16[4,2,4096]{2,1,0:T(2,128)(2,1)} %get-tuple-element.4) | data formatting | bytes 131072
  43.8 0.0 copy-done
  43.8 0.6 %copy.23 = f32[2,1,4]{2,1,0:T(1,128)} copy(f32[2,1,4]{2,1,0:T(1,128)S(1)} %copy-done) | data formatting | bytes 64
Async XLA Ops:
  42.3 1.5 %copy-start = (f32[2,1,4]{2,1,0:T(1,128)S(1)}, f32[2,1,4]{2,1,0:T(1,128)}, u32[]{:S(2)}) copy-start(f32[2,1,4]{2,1,0:T(1,128)} %get-tuple-element.5) | copy-start | bytes 100

commit v4 on v3

--- a/solution.py
+++ b/solution.py
@@ -124,15 +124,31 @@
 
 def kernel(dims, *refs):
     owners, groups, grid, depth, sticks, waves, bands, teams, subs = dims
+    half, rows, wide = grid // 2, groups * 16, 4 * sticks
+    shapes = [
+        (half, waves), (2 * sticks, waves), (2 * bands, 16, waves),
+        (groups, 256, wide), (groups, wide, 256), (groups, 16, wide),
+        (bands, rows, 256), (bands, rows, 256), (2 * bands, rows, 256),
+        (2 * subs, waves), (256, 128), *[ref.shape for ref in refs[10:18]],
+    ]
+    pl.run_scoped(
+        functools.partial(apply, dims, refs), *[pltpu.VMEM(shape, BF16) for shape in shapes]
+    )
+
+
+def apply(dims, refs, *near_refs):
+    owners, groups, grid, depth, sticks, waves, bands, teams, subs = dims
     inputs, (out, inter), refs = refs[:18], refs[18:20], refs[20:]
     prev = inputs[5]
     held, refs = refs[:17], refs[17:]
     orb, slot, column, pot, sub = held[:5]
-    zf, zb, yf, xf, xb, yb = (held[5 + 2 * i : 7 + 2 * i] for i in range(6))
-    (high_hot, low_hot, rep, stage, send, recv, send2, recv2, cols, ymask, ymask_t, xmask,
-     val, gre, gim, back, pots, turn, left, numbers, pall, r1, r2, r3) = refs[:24]
+    zf, zb = held[5:7], held[7:9]
+    (high_hot, low_hot, rep, ymask, ymask_t, xmask, gre, gim, back, left, numbers) = near_refs[:11]
+    fixed = near_refs[11:]
+    yf, xf, xb, yb = (fixed[2 * i : 2 * i + 2] for i in range(4))
+    (stage, send, recv, send2, recv2, cols, val, pots, turn, pall, r1, r2, r3) = refs[:13]
     (in_s, col_s, col_r, fwd_s, first_r, fwd_r, bwd_s, bwd_r, prev_s, prev_r,
-     one_s, one_r, two_s, two_r) = refs[24:]
+     one_s, one_r, two_s, two_r) = refs[13:]
     parts = 2 * bands
     wide = 4 * sticks
     half = grid // 2
@@ -247,6 +263,8 @@
             table = jnp.concatenate([even, odd], axis=0).T[:grid]
             even, odd = sorted_rows(jnp.concatenate([table, side], axis=1))
             pots[z] = jnp.concatenate([even, gap, odd, gap], axis=0).T[:grid]
+        for src, dst in zip(held[9:], fixed, strict=True):
+            dst[...] = src[...]
         left[...] = jnp.concatenate([sub[j] for j in range(subs)], axis=0)
 
     def masks(h):
@@ -469,6 +487,17 @@
         wait_bytes(r1.at[pl.ds(0, teams - 1)], one_s)
 
 
+def deliver(applied, inter, out, sums, sems):
+    copies = [
+        pltpu.make_async_copy(applied, out, sems.at[0]),
+        pltpu.make_async_copy(inter, sums, sems.at[1]),
+    ]
+    for copy in copies:
+        copy.start()
+    for copy in copies:
+        copy.wait()
+
+
 def per_device(orbitals, sphere_slot, stick_column, potential, subspace, previous):
     owners = lax.axis_size("fft")
     teams = lax.axis_size("band")
@@ -496,36 +525,25 @@
     one = pltpu.SemaphoreType.DMA
     four = pltpu.SemaphoreType.DMA((4,))
     several = pltpu.SemaphoreType.DMA((depth,))
-    return tuple(pl.pallas_call(
+    applied, inter = pl.pallas_call(
         functools.partial(kernel, dims),
         out_shape=[
-            jax.ShapeDtypeStruct(orbitals.shape, BF16),
-            jax.ShapeDtypeStruct((2, 1, bands), F32),
+            pltpu.VMEM(orbitals.shape, BF16),
+            pltpu.VMEM((2, 1, bands), F32),
         ],
         in_specs=[pl.BlockSpec(memory_space=pl.ANY) for _ in range(6 + len(every))],
         out_specs=[vmem(), vmem()],
         scratch_shapes=[
             *[pltpu.VMEM(t.shape, t.dtype) for t in given if t is not previous],
-            pltpu.VMEM((half, waves), BF16),
-            pltpu.VMEM((2 * sticks, waves), BF16),
-            pltpu.VMEM((parts, 16, waves), BF16),
             pltpu.VMEM((depth, owners * parts, sticks), F32),
             message,
             message,
             message,
             message,
             pltpu.VMEM((owners, 1, sticks), jnp.int32),
-            pltpu.VMEM((groups, 256, 4 * sticks), BF16),
-            pltpu.VMEM((groups, 4 * sticks, 256), BF16),
-            pltpu.VMEM((groups, 16, 4 * sticks), BF16),
             pltpu.VMEM((groups, parts, 4 * sticks), F32),
-            pltpu.VMEM((bands, groups * 16, 256), BF16),
-            pltpu.VMEM((bands, groups * 16, 256), BF16),
-            pltpu.VMEM((parts, groups * 16, 256), BF16),
             pltpu.VMEM((depth, grid, 256), F32),
             pltpu.VMEM((2, grid, 128), F32),
-            pltpu.VMEM((2 * subs, waves), BF16),
-            pltpu.VMEM((256, 128), BF16),
             pltpu.VMEM((teams, *previous.shape), BF16),
             sums,
             sums,
@@ -537,7 +555,18 @@
             vmem_limit_bytes=60 * 2**20, collective_id=0, has_side_effects=True
         ),
         name="apply",
-    )(*given))
+    )(*given)
+    return tuple(pl.pallas_call(
+        deliver,
+        out_shape=[
+            jax.ShapeDtypeStruct(orbitals.shape, BF16),
+            jax.ShapeDtypeStruct((2, 1, bands), F32),
+        ],
+        in_specs=[vmem(), vmem()],
+        out_specs=[pl.BlockSpec(memory_space=pl.ANY)] * 2,
+        scratch_shapes=[pltpu.SemaphoreType.DMA((2,))],
+        name="deliver",
+    )(pltpu.with_memory_space_constraint(applied, pltpu.VMEM), pltpu.with_memory_space_constraint(inter, pltpu.VMEM)))
 
 
 def solution(mesh):

time: 45.1 us -> 42.6 us (0.945)
  local copies, waits for them, and re-layouts: 2.08 us -> 0 us
    unnamed x4 -> x0, local copies, waits for them, and re-layouts: 2.08 us -> none
    pallas_call x1 -> x2, Pallas kernels: 41.7 us -> 41.4 us  [the longest x1 40.7 us: per_device(): pl.pallas_call(functools.partial(kernel, dims), out_shape=[pltpu.VMEM(orb...]
where the time goes in v4:
time: 42.6 us; the launch traced here: 42 us
  Pallas kernels  41.4 us (97%)
  between operations  0.64 us (2%)
    pallas_call x1, Pallas kernels, per_device(): pl.pallas_call(functools.partial(kernel, dims), out_shape=[pltpu.VMEM(orb...  40.7 us

profile of v4, /device:TPU:8, one launch (start us, length us, event | category | flops | bytes accessed | tf_op | source)
XLA Modules:
  0.0 42.0 jit_solution(15963890419323863176)
XLA Ops:
  0.6 40.7 %apply.1 = (bf16[4,2,4096]{2,1,0:T(2,128)(2,1)S(1)}, f32[2,1,4]{2,1,0:T(1,128)S(1)}) custom-call(bf16[4,2,4096]{2,1,0:T(2,128)(2,1)} %refs_0_.1, s32[1,4096]{1,0:T(1,128)} %bitcast.2, s32[1,128]{1,0:T(1,128)} %bitcast.3, f32[3,192,192]{2,1,0:T(8,128)} %refs_3_.1, bf16[16,2,4096]{2,1,0:T(2,128)(2,1)} %refs_4_.1, bf16[4,2,4096]{2,1,0:T(2,128)(2,1)} %refs_5_.1, ...), custom_call_target="tpu_custom_call" | custom-call | tf_op jit(solution)/shard_map/apply/pallas_call | solution.py:528
  41.3 0.7 %deliver.1 = (bf16[4,2,4096]{2,1,0:T(2,128)(2,1)}, f32[2,1,4]{2,1,0:T(1,128)}) custom-call(bf16[4,2,4096]{2,1,0:T(2,128)(2,1)S(1)} %get-tuple-element.4.applied, f32[2,1,4]{2,1,0:T(1,128)S(1)} %get-tuple-element.5.inter), custom_call_target="tpu_custom_call" | custom-call | tf_op jit(solution)/shard_map/deliver/pallas_call | solution.py:559

commit v5 on v4

--- a/solution.py
+++ b/solution.py
@@ -61,6 +61,10 @@
         made.append(joined(*waves(2 * m + odd, m, -1.0, 1.0 / grid), m, xpos, half, wide).T)
     for odd in range(2):
         made.append(joined(*waves(2 * m + odd, m, -1.0, 1.0 / grid), m, m, lanes, lanes))
+    last = depth * np.arange(owners) + depth - 1
+    made.append(np.concatenate(
+        [t for odd in range(2) for t in waves(last, 2 * m + odd, -1.0, 1.0 / grid)], 0
+    ))
     return [bf16(t) for t in made]
 
 
@@ -129,7 +133,7 @@
         (half, waves), (2 * sticks, waves), (2 * bands, 16, waves),
         (groups, 256, wide), (groups, wide, 256), (groups, 16, wide),
         (bands, rows, 256), (bands, rows, 256), (2 * bands, rows, 256),
-        (2 * subs, waves), (256, 128), *[ref.shape for ref in refs[10:18]],
+        (2 * subs, waves), (256, 128), (sticks, waves), *[ref.shape for ref in refs[10:18]],
     ]
     pl.run_scoped(
         functools.partial(apply, dims, refs), *[pltpu.VMEM(shape, BF16) for shape in shapes]
@@ -138,17 +142,17 @@
 
 def apply(dims, refs, *near_refs):
     owners, groups, grid, depth, sticks, waves, bands, teams, subs = dims
-    inputs, (out, inter), refs = refs[:18], refs[18:20], refs[20:]
+    inputs, (out, inter), refs = refs[:19], refs[19:21], refs[21:]
     prev = inputs[5]
-    held, refs = refs[:17], refs[17:]
+    held, refs = refs[:18], refs[18:]
     orb, slot, column, pot, sub = held[:5]
     zf, zb = held[5:7], held[7:9]
-    (high_hot, low_hot, rep, ymask, ymask_t, xmask, gre, gim, back, left, numbers) = near_refs[:11]
-    fixed = near_refs[11:]
+    (high_hot, low_hot, rep, ymask, ymask_t, xmask, gre, gim, back, left, numbers, shot) = near_refs[:12]
+    fixed = near_refs[12:]
     yf, xf, xb, yb = (fixed[2 * i : 2 * i + 2] for i in range(4))
-    (stage, send, recv, send2, recv2, cols, val, pots, turn, pall, r1, r2, r3) = refs[:13]
+    (stage, send, recv, send2, recv2, cols, val, pots, turn, pall, r1, r2, r3, sofar, swing) = refs[:15]
     (in_s, col_s, col_r, fwd_s, first_r, fwd_r, bwd_s, bwd_r, prev_s, prev_r,
-     one_s, one_r, two_s, two_r) = refs[13:]
+     one_s, one_r, two_s, two_r) = refs[15:]
     parts = 2 * bands
     wide = 4 * sticks
     half = grid // 2
@@ -182,7 +186,7 @@
         fetches[i].start()
     for mate in mates:
         greet("band", mate)
-    for i in (3, 4, *range(7, 17)):
+    for i in (3, 4, *range(7, 18)):
         fetches[i].start()
 
     with jax.named_scope("hots"):
@@ -236,16 +240,16 @@
         for peer in peers:
             start_to(send.at[0, peer], recv.at[0, place], fwd_s.at[0], first_r.at[batch], "fft", peer)
         pltpu.make_async_copy(send.at[0, me], recv.at[0, place], first_r.at[batch]).start()
-        for mate in mates:
-            start_to(prev, pall.at[team], prev_s, prev_r, "band", mate)
-        pltpu.make_async_copy(prev, pall.at[team], prev_r).start()
         for z in range(1, depth):
             for peer in peers:
                 start_to(send.at[z, peer], recv.at[z, place], fwd_s.at[z], fwd_r.at[z], "fft", peer)
             pltpu.make_async_copy(send.at[z, me], recv.at[z, place], fwd_r.at[z]).start()
+        for mate in mates:
+            start_to(prev, pall.at[team], prev_s, prev_r, "band", mate)
+        pltpu.make_async_copy(prev, pall.at[team], prev_r).start()
 
     with jax.named_scope("early"):
-        for i in (3, 4, *range(7, 17)):
+        for i in (3, 4, *range(7, 18)):
             fetches[i].wait()
         side = jnp.zeros((grid, 256 - grid), F32)
         gap = jnp.zeros((128 - half, 256), F32)
@@ -263,7 +267,7 @@
             table = jnp.concatenate([even, odd], axis=0).T[:grid]
             even, odd = sorted_rows(jnp.concatenate([table, side], axis=1))
             pots[z] = jnp.concatenate([even, gap, odd, gap], axis=0).T[:grid]
-        for src, dst in zip(held[9:], fixed, strict=True):
+        for src, dst in zip(held[9:17], fixed, strict=True):
             dst[...] = src[...]
         left[...] = jnp.concatenate([sub[j] for j in range(subs)], axis=0)
 
@@ -343,12 +347,10 @@
         row = lax.broadcasted_iota(jnp.int32, (16, parts * 16), 0)
         ones = (lax.div(line, 16) == row).astype(F32).astype(BF16)
         spots = [(4 * around[o] + k, 4 * k + around[o]) for o in turns for k in range(4)]
-        tall = []
+        cut = []
         for h, g in spots:
             at = pl.ds(pl.multiple_of(16 * g, 16), 16)
-            tall.append(dot(back[:, at, :].reshape(parts * 16, 256), ymask[h]))
-        cut = []
-        for t, (h, g) in zip(tall, spots, strict=True):
+            t = dot(back[:, at, :].reshape(parts * 16, 256), ymask[h])
             t = t.astype(BF16).reshape(parts, 16, wide) * xmask[h][None]
             cut.append(t.reshape(parts * 16, wide))
         for t, (h, g) in zip(cut, spots, strict=True):
@@ -390,10 +392,6 @@
         pltpu.make_async_copy(r1.at[team], r2.at[team], one_r).start()
 
     def first(i, carry):
-        @pl.when(i == 3)
-        def _():
-            overlaps()
-
         q = lax.rem(batch + near(i), 4)
         wait_bytes(cols.at[pl.ds(16 * q, 16)], col_r.at[q])
         for k in range(4):
@@ -420,6 +418,10 @@
 
         work(z)
 
+        @pl.when(z == 0)
+        def _():
+            overlaps()
+
         return carry
 
     lax.fori_loop(0, depth, plane, 0)
@@ -439,16 +441,25 @@
         y = col - x * grid
         coords = jnp.concatenate([x, y, x, y, x, y, x, y], axis=0).astype(F32).astype(BF16)
         coords = jnp.concatenate([coords, coords], axis=1)
-        for z in range(depth):
+        shot[...] = low_hot[:sticks] + low_hot[sticks:]
+
+        def unpack(z):
             wait_bytes(recv2.at[z], bwd_r.at[z])
             for f in range(owners):
                 stage[z, parts * f : parts * (f + 1), :] = recv2[z, f].astype(F32)
+
+        def column_of(z, p, b):
+            return stage[z, pl.ds(p * bands + b, owners, stride=parts), :].astype(BF16)
+
+        for z in range(depth - 1):
+            unpack(z)
     with jax.named_scope("zback"):
+        nothing = jnp.zeros((owners, sticks), BF16)
         lines = []
         for b in range(bands):
             field = jnp.concatenate(
-                [stage[z, pl.ds(p * bands + b, owners, stride=parts), :].astype(BF16)
-                 for p in range(2) for z in range(depth)], axis=0
+                [piece for p in range(2)
+                 for piece in [*[column_of(z, p, b) for z in range(depth - 1)], nothing]], axis=0
             )
             for p in range(2):
                 done = dot(zb[p][...], field).astype(BF16)
@@ -467,9 +478,34 @@
             t = dot(lines, low_cut).reshape(parts, half, chunk)
             got = jnp.sum(t * high_hot[:, cut].astype(F32)[None], axis=1)
             for b in range(bands):
-                out[b, :, cut] = (
+                sofar[2 * b : 2 * b + 2, cut] = (
                     got[2 * b : 2 * b + 2] + kinetic * orb[b, :, cut].astype(F32)
-                ).astype(BF16)
+                )
+            turns = dot(held[17][...], high_hot[:, cut])
+            even = lax.rem(plane_at, 2) == 0
+            for p in range(2):
+                swing[p, :, cut] = jnp.where(
+                    even,
+                    turns[p * owners : (p + 1) * owners],
+                    turns[(2 + p) * owners : (3 + p) * owners],
+                )
+    with jax.named_scope("last"):
+        unpack(depth - 1)
+        field = jnp.concatenate(
+            [column_of(depth - 1, p, b) for b in range(bands) for p in range(2)], axis=0
+        )
+        for c in range(0, waves, chunk):
+            cut = slice(c, c + chunk)
+            t = dot(field, shot[:, cut])
+            wr, wi = swing[0, :, cut], swing[1, :, cut]
+            for b in range(bands):
+                re = t[2 * b * owners : (2 * b + 1) * owners]
+                im = t[(2 * b + 1) * owners : (2 * b + 2) * owners]
+                got = jnp.concatenate(
+                    [jnp.sum(re * wr - im * wi, axis=0, keepdims=True),
+                     jnp.sum(re * wi + im * wr, axis=0, keepdims=True)], axis=0
+                )
+                out[b, :, cut] = (sofar[2 * b : 2 * b + 2, cut] + got).astype(BF16)
 
     with jax.named_scope("waits"):
         wait_bytes(r3, two_r)
@@ -548,7 +584,9 @@
             sums,
             sums,
             pltpu.VMEM((owners, 2, 128), F32),
-            pltpu.SemaphoreType.DMA((17,)),
+            pltpu.VMEM((parts, waves), F32),
+            pltpu.VMEM((2, owners, waves), F32),
+            pltpu.SemaphoreType.DMA((18,)),
             one, four, several, four, several, several, several, one, one, one, one, one, one,
         ],
         compiler_params=pltpu.CompilerParams(

time: 42.6 us -> 42.1 us (0.988)
  Pallas kernels: 41.4 us -> 40.7 us
    pallas_call x1, Pallas kernels: 40.7 us -> 40.1 us  [per_device(): pl.pallas_call(functools.partial(kernel, dims), out_shape=[pltpu.VMEM(orb...]
where the time goes in v5:
time: 42.1 us; the launch traced here: 41.5 us
  Pallas kernels  40.7 us (97%)
  between operations  0.8 us (2%)
    pallas_call x1, Pallas kernels, per_device(): pl.pallas_call(functools.partial(kernel, dims), out_shape=[pltpu.VMEM(orb...  40.1 us

profile of v5, /device:TPU:8, one launch (start us, length us, event | category | flops | bytes accessed | tf_op | source)
XLA Modules:
  0.0 41.5 jit_solution(15356183793348647953)
XLA Ops:
  0.6 40.1 %apply.1 = (bf16[4,2,4096]{2,1,0:T(2,128)(2,1)S(1)}, f32[2,1,4]{2,1,0:T(1,128)S(1)}) custom-call(bf16[4,2,4096]{2,1,0:T(2,128)(2,1)} %refs_0_.1, s32[1,4096]{1,0:T(1,128)} %bitcast.2, s32[1,128]{1,0:T(1,128)} %bitcast.3, f32[3,192,192]{2,1,0:T(8,128)} %refs_3_.1, bf16[16,2,4096]{2,1,0:T(2,128)(2,1)} %refs_4_.1, bf16[4,2,4096]{2,1,0:T(2,128)(2,1)} %refs_5_.1, ...), custom_call_target="tpu_custom_call" | custom-call | tf_op jit(solution)/shard_map/apply/pallas_call | solution.py:564
  40.7 0.7 %deliver.1 = (bf16[4,2,4096]{2,1,0:T(2,128)(2,1)}, f32[2,1,4]{2,1,0:T(1,128)}) custom-call(bf16[4,2,4096]{2,1,0:T(2,128)(2,1)S(1)} %get-tuple-element.4.applied, f32[2,1,4]{2,1,0:T(1,128)S(1)} %get-tuple-element.5.inter), custom_call_target="tpu_custom_call" | custom-call | tf_op jit(solution)/shard_map/deliver/pallas_call | solution.py:597
